TPU v7x, 32 devices: a whole 2x2x4 slice. The times are simulated.
32 devices in a mesh: grp: 8 (over y, x, core), mem: 4 (over z).
Axes of the slice: x: 2, y: 2, z: 4, core: 2. Of those that a mesh axis runs over, the one named last changes fastest.
Arguments:
- residual: float32 [256, 64, 256], P(('grp', 'mem')), may hold values from -6 to 6
- direction: float32 [256, 64, 256], P(('grp', 'mem')), may hold values from -6 to 6
- local_inverse: bfloat16 [256, 256, 256], P(('grp', 'mem')), may hold values from -1 to 16, as said below
- dirichlet: bfloat16 [256, 256, 256], P(('grp', 'mem')), may hold values from -1 to 16, as said below
- coupling: bfloat16 [256, 24, 256], P(('grp', 'mem')), may hold values from -0.375 to 0.375
- corner_map: int32 [256, 24], P(('grp', 'mem')), may hold values from 0 to 6143
- coarse_factor: bfloat16 [8, 2048, 2048], P('grp'), may hold values from -1 to 3, as said below
Outputs:
- new_residual: float32 [256, 64, 256], P(('grp', 'mem'))
- new_direction: float32 [256, 64, 256], P(('grp', 'mem'))
- step_sizes: float32 [3, 64], replicated
Inputs may be any that keep to these rules, and one draw needn't show every extreme that they name: `local_inverse`: each subdomain's matrix is symmetric positive definite. `dirichlet`: each subdomain's matrix is symmetric positive definite. `coarse_factor`: each group's factor is lower triangular with a positive diagonal.
All inputs are finite; a program needn't handle non-finite values.
Results may differ from a plain program's by a relative error of at most 0.0083.
Values sent between devices are 32-bit elements; how exact they have to be, the bound alone decides.
A program may use at most 128 MiB of HBM per device.

v0:
```python
import jax
import jax.numpy as jnp
from jax import lax
from jax.sharding import PartitionSpec as P

ITERS = 3
highest = lax.Precision.HIGHEST


def from_behind(block, axis, distance):
    devices = range(lax.axis_size(axis))
    route = [((i - distance) % len(devices), i) for i in devices]
    return lax.ppermute(block, axis, route)


def extended(cells, sides, width):
    for axis, dim in sides:
        count = lax.axis_size(axis)
        head = lax.slice_in_dim(cells, 0, width, axis=dim)
        tail = lax.slice_in_dim(cells, cells.shape[dim] - width, cells.shape[dim], axis=dim)
        cells = jnp.concatenate(
            [
                lax.ppermute(tail, axis, [(i, (i + 1) % count) for i in range(count)]),
                cells,
                lax.ppermute(head, axis, [((i + 1) % count, i) for i in range(count)]),
            ],
            axis=dim,
        )
    return cells


def solve_local(matrices, vectors):
    return jnp.einsum(
        "sij,skj->ski", matrices, vectors.astype(jnp.bfloat16), preferred_element_type=jnp.float32
    )


def column_sums(left_side, right_side):
    return jnp.sum(left_side * right_side, axis=(0, 2))


def coarse_solve(factor, coarse_load):
    forward = jax.scipy.linalg.solve_triangular(factor, coarse_load.T, lower=True)
    return jax.scipy.linalg.solve_triangular(factor, forward, lower=True, trans=1).T


def fold_neighbours(partial_value, block_size):
    from_upper = from_behind(partial_value[:, :block_size], "grp", -1)
    from_lower = from_behind(partial_value[:, 2 * block_size :], "grp", 1)
    return partial_value[:, block_size : 2 * block_size] + from_upper + from_lower


def local(residual, direction, local_inverse, dirichlet, coupling, corner_map, coarse_factor):
    sub_count, rhs_count, dofs_count = residual.shape
    corner_count = coupling.shape[1]
    block_size = coarse_factor.shape[1]
    factor = coarse_factor[0].astype(jnp.float32)
    flat_map = corner_map.reshape(-1)
    coupling_wide = coupling.astype(jnp.float32)
    precond = solve_local(dirichlet, residual)
    norm_now = lax.psum(column_sums(residual, precond), ("grp", "mem"))
    step_list = []
    for iteration in range(ITERS):
        solved = solve_local(local_inverse, direction)
        partial_corner = jnp.einsum("ski,sci->skc", solved, coupling_wide, precision=highest)
        flat_corner = partial_corner.transpose(1, 0, 2).reshape(rhs_count, sub_count * corner_count)
        partial_value = (
            jnp.zeros((rhs_count, 3 * block_size), jnp.float32).at[:, flat_map].add(flat_corner)
        )
        folded = fold_neighbours(partial_value, block_size)
        solution = coarse_solve(factor, lax.psum(folded, "mem"))
        widened = extended(solution, (("grp", 1),), block_size)
        picked = widened[:, flat_map].reshape(rhs_count, sub_count, corner_count).transpose(1, 0, 2)
        lifted = jnp.einsum("skc,sci->ski", picked, coupling_wide, precision=highest)
        image = solve_local(local_inverse, direction + lifted)
        curvature = lax.psum(column_sums(direction, image), ("grp", "mem"))
        alpha = norm_now / curvature
        step_list.append(alpha)
        residual = residual - alpha[None, :, None] * image
        precond = solve_local(dirichlet, residual)
        norm_next = lax.psum(column_sums(residual, precond), ("grp", "mem"))
        direction = precond + (norm_next / norm_now)[None, :, None] * direction
        norm_now = norm_next
    return (residual, direction, jnp.stack(step_list))


def solution(mesh):
    return jax.shard_map(
        local,
        mesh=mesh,
        in_specs=(
            P(("grp", "mem"), None, None),
            P(("grp", "mem"), None, None),
            P(("grp", "mem"), None, None),
            P(("grp", "mem"), None, None),
            P(("grp", "mem"), None, None),
            P(("grp", "mem"), None),
            P("grp", None, None),
        ),
        out_specs=(P(("grp", "mem"), None, None), P(("grp", "mem"), None, None), P()),
        check_vma=False,
    )
```

profile of v0, /device:TPU:0, one launch (start us, length us, event | category | flops | bytes accessed | tf_op | source)
XLA Modules:
  0.0 917.9 jit_solution(7679273841835778049)
XLA Ops:
  11.1 3.0 scatter_custom_fusion
  14.1 3.0 fusion.365
  24.0 11.3 %convert_select_fusion = f32[2048,2048]{1,0:T(8,128)} fusion(bf16[1,2048,2048]{2,1,0:T(8,128)(2,1)} %param.17), kind=kLoop, calls=%fused_computation.8 | loop fusion | flops 12582912 | bytes 25165824 | tf_op jit(solution)/shard_map/jit(_solve_triangular)/triangular_solve | solution.py:44
  37.6 55.7 %while.12 = (s32[]{:T(128)}, f32[2048,2048]{1,0:T(8,128)}, s32[16,2]{0,1:T(2,128)S(1)}, f32[16,128,128]{2,1,0:T(8,128)}, s32[]{:T(128)}) while((s32[]{:T(128)}, f32[2048,2048]{1,0:T(8,128)}, s32[16,2]{0,1:T(2,128)S(1)}, f32[16,128,128]{2,1,0:T(8,128)}, s32[]{:T(128)}) %tuple.417), condition=%wide.while_cond.1, body=%wide.while_body.1.sunk | while | flops 2 | bytes 132205 | solution.py:44
  93.3 158.4 %custom-call.11 = f32[16,128,128]{1,2,0:T(8,128)S(1)} custom-call(f32[16,128,128]{2,1,0:T(8,128)} %get-tuple-element.46), custom_call_target="InvertDiagBlocksLowerTriangular" | custom-call | tf_op jit(solution)/shard_map/jit(_solve_triangular)/triangular_solve | solution.py:44
  308.3 11.7 %collective-permute-done.3 = f32[64,2048]{1,0:T(8,128)S(1)} collective-permute-done((f32[64,2048]{1,0:T(8,128)S(1)}, f32[64,2048]{1,0:T(8,128)S(1)}, u32[]{:S(2)}, u32[]{:S(2)}) %collective-permute-start.3) | collective-permute-done | bytes 524320 | tf_op jit(solution)/shard_map/ppermute | solution.py:25
  322.5 3.2 copy.31
  332.1 39.5 %all-reduce = (f32[64]{0:T(128)S(1)}, f32[64]{0:T(128)S(1)}) all-reduce(f32[64]{0:T(128)S(1)} %fusion.9, f32[64]{0:T(128)S(1)} %get-tuple-element.437), channel_id=1, replica_groups=mesh['grp'=8,'mem'=4] {'grp','mem'}, use_global_device_ids=true, to_apply=%region_1.0 | all-reduce | flops 128 | bytes 1024 | tf_op jit(solution)/shard_map/psum | solution.py:61
  375.1 40.9 %psum.73 = f32[64]{0:T(128)S(1)} all-reduce(f32[64]{0:T(128)S(1)} %get-tuple-element.439), channel_id=1, replica_groups=mesh['grp'=8,'mem'=4] {'grp','mem'}, use_global_device_ids=true, to_apply=%region_7.0 | all-reduce | flops 64 | bytes 512 | tf_op jit(solution)/shard_map/psum | solution.py:81
  422.0 3.6 fusion.364
  435.3 8.7 collective-permute-done.5
  447.3 38.6 %all-reduce.7.cloned.1.call-done = f32[2048,64]{0,1:T(8,128)} async-done(((f32[2048,64]{0,1:T(8,128)}), f32[2048,64]{0,1:T(8,128)}) %all-reduce.7.cloned.1.call-update) | async-done | bytes 524304 | tf_op jit(solution)/shard_map/psum | solution.py:71
  556.5 12.2 %collective-permute-done.7 = f32[64,2048]{1,0:T(8,128)S(1)} collective-permute-done((f32[64,2048]{1,0:T(8,128)S(1)}, f32[64,2048]{1,0:T(8,128)S(1)}, u32[]{:S(2)}, u32[]{:S(2)}) %collective-permute-start.7) | collective-permute-done | bytes 524320 | tf_op jit(solution)/shard_map/ppermute | solution.py:25
  572.0 3.2 copy.35
  581.7 39.3 %psum.75 = f32[64]{0:T(128)S(1)} all-reduce(f32[64]{0:T(128)S(1)} %get-tuple-element.479), channel_id=1, replica_groups=mesh['grp'=8,'mem'=4] {'grp','mem'}, use_global_device_ids=true, to_apply=%region_11.0 | all-reduce | flops 64 | bytes 512 | tf_op jit(solution)/shard_map/psum | solution.py:76
  624.5 38.9 %psum.76 = f32[64]{0:T(128)S(1)} all-reduce(f32[64]{0:T(128)S(1)} %get-tuple-element.481), channel_id=1, replica_groups=mesh['grp'=8,'mem'=4] {'grp','mem'}, use_global_device_ids=true, to_apply=%region_13.0 | all-reduce | flops 64 | bytes 512 | tf_op jit(solution)/shard_map/psum | solution.py:81
  666.4 3.0 scatter_custom_fusion.2
  669.4 3.6 fusion.363
  682.9 7.5 collective-permute-done.9
  694.3 39.1 %all-reduce.9.cloned.1.call-done = f32[2048,64]{0,1:T(8,128)} async-done(((f32[2048,64]{0,1:T(8,128)}), f32[2048,64]{0,1:T(8,128)}) %all-reduce.9.cloned.1.call-update) | async-done | bytes 524304 | tf_op jit(solution)/shard_map/psum | solution.py:71
  804.0 12.3 %collective-permute-done.11 = f32[64,2048]{1,0:T(8,128)S(1)} collective-permute-done((f32[64,2048]{1,0:T(8,128)S(1)}, f32[64,2048]{1,0:T(8,128)S(1)}, u32[]{:S(2)}, u32[]{:S(2)}) %collective-permute-start.11) | collective-permute-done | bytes 524320 | tf_op jit(solution)/shard_map/ppermute | solution.py:25
  819.5 3.2 copy.39
  828.4 39.3 %psum.78 = f32[64]{0:T(128)S(1)} all-reduce(f32[64]{0:T(128)S(1)} %get-tuple-element.521), channel_id=1, replica_groups=mesh['grp'=8,'mem'=4] {'grp','mem'}, use_global_device_ids=true, to_apply=%region_17.0 | all-reduce | flops 64 | bytes 512 | tf_op jit(solution)/shard_map/psum | solution.py:76
  869.4 38.9 %psum.79 = f32[64]{0:T(128)S(1)} all-reduce(f32[64]{0:T(128)S(1)} %get-tuple-element.523), channel_id=1, replica_groups=mesh['grp'=8,'mem'=4] {'grp','mem'}, use_global_device_ids=true, to_apply=%region_19.0 | all-reduce | flops 64 | bytes 512 | tf_op jit(solution)/shard_map/psum | solution.py:81
  (676 shorter events, 337.1 us)
Async XLA Ops:
  7.2 1.2 copy-start
  7.2 244.6 %all-reduce.5.cloned.1.call-start = ((), (), s32[]{:S(2)}) async-start(), calls=%async_computation | async-start | bytes 1048576 | tf_op jit(solution)/shard_map/psum | solution.py:71
  19.5 16.1 %collective-permute-start.1 = (f32[64,2048]{1,0:T(8,128)}, f32[64,2048]{1,0:T(8,128)}, u32[]{:S(2)}, u32[]{:S(2)}) collective-permute-start(f32[64,2048]{1,0:T(8,128)} %copy.30), channel_id=1, source_target_pairs={{28,0},{0,4},{4,8},{8,12},{12,16},{16,20},{20,24},{24,28},{29,1},{... | collective-permute-start | bytes 1572872 | tf_op jit(solution)/shard_map/ppermute | solution.py:13
  21.1 14.5 %collective-permute-start = (f32[64,2048]{1,0:T(8,128)}, f32[64,2048]{1,0:T(8,128)S(1)}, u32[]{:S(2)}, u32[]{:S(2)}) collective-permute-start(f32[64,2048]{1,0:T(8,128)} %copy.29), channel_id=1, source_target_pairs={{4,0},{8,4},{12,8},{16,12},{20,16},{24,20},{28,24},{0,28},{5,1},{9... | collective-permute-start | bytes 1572872 | tf_op jit(solution)/shard_map/ppermute | solution.py:13
  37.6 448.3 %all-reduce.7.cloned.1.call-start = ((), (), s32[]{:S(2)}) async-start(), calls=%async_computation.1 | async-start | bytes 1048576 | tf_op jit(solution)/shard_map/psum | solution.py:71
  251.8 39.4 %copy-start.1 = (f32[2048,2048]{1,0:T(8,128)S(1)}, f32[2048,2048]{1,0:T(8,128)}, u32[]{:S(2)}) copy-start(f32[2048,2048]{1,0:T(8,128)} %get-tuple-element.572) | copy-start | bytes 50331652
  272.1 35.6 %copy-start.2 = (bf16[8,256,256]{2,1,0:T(8,128)(2,1)S(1)}, bf16[8,256,256]{2,1,0:T(8,128)(2,1)}, u32[]{:S(2)}) copy-start(bf16[8,256,256]{2,1,0:T(8,128)(2,1)} %param.14) | copy-start | bytes 3145732
  272.1 35.6 %copy-start.9 = (f32[8,64,256]{2,1,0:T(8,128)S(1)}, f32[8,64,256]{2,1,0:T(8,128)}, u32[]{:S(2)}) copy-start(f32[8,64,256]{2,1,0:T(8,128)} %param.11) | copy-start | bytes 1572868
  292.3 35.9 %copy-start.7 = (bf16[8,24,256]{2,1,0:T(8,128)(2,1)S(1)}, bf16[8,24,256]{2,1,0:T(8,128)(2,1)}, u32[]{:S(2)}) copy-start(bf16[8,24,256]{2,1,0:T(8,128)(2,1)} %param.15) | copy-start | bytes 294916
  306.0 13.9 %collective-permute-start.3 = (f32[64,2048]{1,0:T(8,128)S(1)}, f32[64,2048]{1,0:T(8,128)S(1)}, u32[]{:S(2)}, u32[]{:S(2)}) collective-permute-start(f32[64,2048]{1,0:T(8,128)S(1)} %bitcast.583), channel_id=1, source_target_pairs={{4,0},{8,4},{12,8},{16,12},{20,16},{24,20},{28,24},{0,28},{5,1},{9... | collective-permute-start | bytes 1572872 | tf_op jit(solution)/shard_map/ppermute | solution.py:25
  307.7 13.5 %collective-permute-start.2 = (f32[64,2048]{1,0:T(8,128)S(1)}, f32[64,2048]{1,0:T(8,128)S(1)}, u32[]{:S(2)}, u32[]{:S(2)}) collective-permute-start(f32[64,2048]{1,0:T(8,128)S(1)} %bitcast.584), channel_id=1, source_target_pairs={{0,4},{4,8},{8,12},{12,16},{16,20},{20,24},{24,28},{28,0},{1,5},{5... | collective-permute-start | bytes 1572872 | tf_op jit(solution)/shard_map/ppermute | solution.py:23
  373.0 0.8 copy-start.6
  417.4 0.8 copy-start.4
  430.3 13.7 %collective-permute-start.5 = (f32[64,2048]{1,0:T(8,128)}, f32[64,2048]{1,0:T(8,128)}, u32[]{:S(2)}, u32[]{:S(2)}) collective-permute-start(f32[64,2048]{1,0:T(8,128)} %copy.34), channel_id=1, source_target_pairs={{28,0},{0,4},{4,8},{8,12},{12,16},{16,20},{20,24},{24,28},{29,1},{... | collective-permute-start | bytes 1572872 | tf_op jit(solution)/shard_map/ppermute | solution.py:13
  430.3 14.3 %collective-permute-start.4 = (f32[64,2048]{1,0:T(8,128)}, f32[64,2048]{1,0:T(8,128)}, u32[]{:S(2)}, u32[]{:S(2)}) collective-permute-start(f32[64,2048]{1,0:T(8,128)} %copy.33), channel_id=1, source_target_pairs={{4,0},{8,4},{12,8},{16,12},{20,16},{24,20},{28,24},{0,28},{5,1},{9... | collective-permute-start | bytes 1572872 | tf_op jit(solution)/shard_map/ppermute | solution.py:13
  446.9 286.5 %all-reduce.9.cloned.1.call-start = ((), (), s32[]{:S(2)}) async-start(), calls=%async_computation.2 | async-start | bytes 1048576 | tf_op jit(solution)/shard_map/psum | solution.py:71
  555.6 13.2 %collective-permute-start.7 = (f32[64,2048]{1,0:T(8,128)S(1)}, f32[64,2048]{1,0:T(8,128)S(1)}, u32[]{:S(2)}, u32[]{:S(2)}) collective-permute-start(f32[64,2048]{1,0:T(8,128)S(1)} %bitcast.586), channel_id=1, source_target_pairs={{4,0},{8,4},{12,8},{16,12},{20,16},{24,20},{28,24},{0,28},{5,1},{9... | collective-permute-start | bytes 1572872 | tf_op jit(solution)/shard_map/ppermute | solution.py:25
  556.5 14.3 %collective-permute-start.6 = (f32[64,2048]{1,0:T(8,128)S(1)}, f32[64,2048]{1,0:T(8,128)S(1)}, u32[]{:S(2)}, u32[]{:S(2)}) collective-permute-start(f32[64,2048]{1,0:T(8,128)S(1)} %bitcast.587), channel_id=1, source_target_pairs={{0,4},{4,8},{8,12},{12,16},{16,20},{20,24},{24,28},{28,0},{1,5},{5... | collective-permute-start | bytes 1572872 | tf_op jit(solution)/shard_map/ppermute | solution.py:23
  622.4 0.8 copy-start.5
  677.7 12.7 %collective-permute-start.9 = (f32[64,2048]{1,0:T(8,128)}, f32[64,2048]{1,0:T(8,128)}, u32[]{:S(2)}, u32[]{:S(2)}) collective-permute-start(f32[64,2048]{1,0:T(8,128)} %copy.38), channel_id=1, source_target_pairs={{28,0},{0,4},{4,8},{8,12},{12,16},{16,20},{20,24},{24,28},{29,1},{... | collective-permute-start | bytes 1572872 | tf_op jit(solution)/shard_map/ppermute | solution.py:13
  677.7 14.3 %collective-permute-start.8 = (f32[64,2048]{1,0:T(8,128)}, f32[64,2048]{1,0:T(8,128)}, u32[]{:S(2)}, u32[]{:S(2)}) collective-permute-start(f32[64,2048]{1,0:T(8,128)} %copy.37), channel_id=1, source_target_pairs={{4,0},{8,4},{12,8},{16,12},{20,16},{24,20},{28,24},{0,28},{5,1},{9... | collective-permute-start | bytes 1572872 | tf_op jit(solution)/shard_map/ppermute | solution.py:13
  803.1 13.2 %collective-permute-start.11 = (f32[64,2048]{1,0:T(8,128)S(1)}, f32[64,2048]{1,0:T(8,128)S(1)}, u32[]{:S(2)}, u32[]{:S(2)}) collective-permute-start(f32[64,2048]{1,0:T(8,128)S(1)} %bitcast.580), channel_id=1, source_target_pairs={{4,0},{8,4},{12,8},{16,12},{20,16},{24,20},{28,24},{0,28},{5,1},{9... | collective-permute-start | bytes 1572872 | tf_op jit(solution)/shard_map/ppermute | solution.py:25
  804.0 14.3 %collective-permute-start.10 = (f32[64,2048]{1,0:T(8,128)S(1)}, f32[64,2048]{1,0:T(8,128)S(1)}, u32[]{:S(2)}, u32[]{:S(2)}) collective-permute-start(f32[64,2048]{1,0:T(8,128)S(1)} %bitcast.581), channel_id=1, source_target_pairs={{0,4},{4,8},{8,12},{12,16},{16,20},{20,24},{24,28},{28,0},{1,5},{5... | collective-permute-start | bytes 1572872 | tf_op jit(solution)/shard_map/ppermute | solution.py:23
  868.9 42.0 %copy-start.8 = (f32[8,64,256]{2,1,0:T(8,128)}, f32[8,64,256]{2,1,0:T(8,128)S(1)}, u32[]{:S(2)}) copy-start(f32[8,64,256]{2,1,0:T(8,128)S(1)} %multiply_subtract_fusion) | copy-start | bytes 1572868
  (1 other events, 0.8 us)
Sparse Core Ops, SparseCore 0:
  37.7 39.7 all-reduce.4
  447.0 38.8 all-reduce.6
  694.4 38.9 all-reduce.8
where the time goes:
time: 931 us; the launch traced here: 918 us
  blocking collectives  237 us (25%)
  matrix products  207 us (22%)
  other arithmetic  198 us (21%)
  waiting for transfers between devices  138 us (15%)
  local copies, waits for them, and re-layouts  107 us (11%)
  between operations  18.2 us (2%)
  starting transfers between devices  12.9 us (1%)
    another operation x4, other arithmetic, coarse_solve(): jax.scipy.linalg.solve_triangular(factor, forward, lower=True, trans=1)  170 us
    another operation x93, matrix products, coarse_solve(): jax.scipy.linalg.solve_triangular(factor, coarse_load.T, lower=True)  124 us
    psum x3, blocking collectives, local(): norm_next = lax.psum(column_sums(residual, precond), ('grp', 'mem'))  119 us
    psum x2, blocking collectives, local(): curvature = lax.psum(column_sums(direction, image), ('grp', 'mem'))  78.5 us
    psum x3, waiting for transfers between devices, local(): solution = coarse_solve(factor, lax.psum(folded, 'mem'))  77.7 us
    another operation x93, matrix products, coarse_solve(): jax.scipy.linalg.solve_triangular(factor, forward, lower=True, trans=1)  64.3 us
    another operation x85, local copies, waits for them, and re-layouts, coarse_solve(): jax.scipy.linalg.solve_triangular(factor, forward, lower=True, trans=1)  55.9 us
    psum x1, blocking collectives, local(): norm_now = lax.psum(column_sums(residual, precond), ('grp', 'mem'))  39.5 us
  transfers between devices with their start and end apart: 15, of which 12 were waited for; matrix products, arithmetic and copies ran while one was open for 25% of the time, Pallas kernels for 0%

commit v1 on v0

--- a/solution.py
+++ b/solution.py
@@ -2,6 +2,7 @@
 import jax.numpy as jnp
 from jax import lax
 from jax.sharding import PartitionSpec as P
+from jax.lax import psum
 
 ITERS = 3
 highest = lax.Precision.HIGHEST
@@ -78,7 +79,8 @@
         step_list.append(alpha)
         residual = residual - alpha[None, :, None] * image
         precond = solve_local(dirichlet, residual)
-        norm_next = lax.psum(column_sums(residual, precond), ("grp", "mem"))
+        in_array = column_sums(residual, precond)
+        norm_next = psum(psum(in_array, axis_name="mem"), axis_name="grp")
         direction = precond + (norm_next / norm_now)[None, :, None] * direction
         norm_now = norm_next
     return (residual, direction, jnp.stack(step_list))

time: 931 us -> 877 us (0.942)
  blocking collectives: 237 us -> 185 us
    psum x3 -> x6, blocking collectives: 119 us -> 66.4 us  [local(): norm_next = psum(psum(in_array, axis_name='mem'), axis_name='grp')]
  transfers between devices with their start and end apart: 15 -> 15, of which waited for: 12 -> 10; matrix products, arithmetic and copies ran while one was open for 25% -> 27% of each run, Pallas kernels for 0% -> 0%
where the time goes in v1:
time: 877 us; the launch traced here: 864 us
  matrix products  207 us (24%)
  other arithmetic  198 us (23%)
  blocking collectives  185 us (21%)
  waiting for transfers between devices  134 us (15%)
  local copies, waits for them, and re-layouts  110 us (13%)
  between operations  18 us (2%)
  starting transfers between devices  12.7 us (1%)
    another operation x4, other arithmetic, coarse_solve(): jax.scipy.linalg.solve_triangular(factor, forward, lower=True, trans=1)  170 us
    another operation x93, matrix products, coarse_solve(): jax.scipy.linalg.solve_triangular(factor, coarse_load.T, lower=True)  124 us
    psum x2, blocking collectives, local(): curvature = lax.psum(column_sums(direction, image), ('grp', 'mem'))  78.5 us
    psum x3, waiting for transfers between devices, local(): solution = coarse_solve(factor, lax.psum(folded, 'mem'))  73.5 us
    psum x6, blocking collectives, local(): norm_next = psum(psum(in_array, axis_name='mem'), axis_name='grp')  66.4 us
    another operation x93, matrix products, coarse_solve(): jax.scipy.linalg.solve_triangular(factor, forward, lower=True, trans=1)  64.4 us
    another operation x85, local copies, waits for them, and re-layouts, coarse_solve(): jax.scipy.linalg.solve_triangular(factor, forward, lower=True, trans=1)  58.1 us
    psum x1, blocking collectives, local(): norm_now = lax.psum(column_sums(residual, precond), ('grp', 'mem'))  39.5 us
  transfers between devices with their start and end apart: 15, of which 10 were waited for; matrix products, arithmetic and copies ran while one was open for 27% of the time, Pallas kernels for 0%

profile of v1, /device:TPU:0, one launch (start us, length us, event | category | flops | bytes accessed | tf_op | source)
XLA Modules:
  0.0 863.7 jit_solution(17691947418626368432)
XLA Ops:
  24.0 11.3 %convert_select_fusion = f32[2048,2048]{1,0:T(8,128)} fusion(bf16[1,2048,2048]{2,1,0:T(8,128)(2,1)} %param.17), kind=kLoop, calls=%fused_computation.8 | loop fusion | flops 12582912 | bytes 25165824 | tf_op jit(solution)/shard_map/jit(_solve_triangular)/triangular_solve | solution.py:45
  37.6 58.0 %while.12 = (s32[]{:T(128)}, f32[2048,2048]{1,0:T(8,128)}, s32[16,2]{0,1:T(2,128)S(1)}, f32[16,128,128]{2,1,0:T(8,128)}, s32[]{:T(128)}) while((s32[]{:T(128)}, f32[2048,2048]{1,0:T(8,128)}, s32[16,2]{0,1:T(2,128)S(1)}, f32[16,128,128]{2,1,0:T(8,128)}, s32[]{:T(128)}) %tuple.417), condition=%wide.while_cond.1, body=%wide.while_body.1.sunk | while | flops 2 | bytes 132205 | solution.py:45
  95.6 158.4 %custom-call.11 = f32[16,128,128]{1,2,0:T(8,128)S(1)} custom-call(f32[16,128,128]{2,1,0:T(8,128)} %get-tuple-element.46), custom_call_target="InvertDiagBlocksLowerTriangular" | custom-call | tf_op jit(solution)/shard_map/jit(_solve_triangular)/triangular_solve | solution.py:45
  310.6 11.7 %collective-permute-done.3 = f32[64,2048]{1,0:T(8,128)S(1)} collective-permute-done((f32[64,2048]{1,0:T(8,128)S(1)}, f32[64,2048]{1,0:T(8,128)S(1)}, u32[]{:S(2)}, u32[]{:S(2)}) %collective-permute-start.3) | collective-permute-done | bytes 524320 | tf_op jit(solution)/shard_map/ppermute | solution.py:26
  324.7 3.2 copy.31
  334.4 39.5 %all-reduce = (f32[64]{0:T(128)S(1)}, f32[64]{0:T(128)S(1)}) all-reduce(f32[64]{0:T(128)S(1)} %fusion.9, f32[64]{0:T(128)S(1)} %get-tuple-element.437), channel_id=1, replica_groups=mesh['grp'=8,'mem'=4] {'grp','mem'}, use_global_device_ids=true, to_apply=%region_1.0 | all-reduce | flops 128 | bytes 1024 | tf_op jit(solution)/shard_map/psum | solution.py:62
  377.4 10.6 %psum.94 = f32[64]{0:T(128)S(1)} all-reduce(f32[64]{0:T(128)S(1)} %get-tuple-element.439), channel_id=1, replica_groups=mesh['grp'=8,'mem'=4] {'mem'}, use_global_device_ids=true, to_apply=%region_7.0 | all-reduce | flops 64 | bytes 512 | tf_op jit(solution)/shard_map/psum | solution.py:83
  388.0 11.9 %psum.95 = f32[64]{0:T(128)S(1)} all-reduce(f32[64]{0:T(128)S(1)} %psum.94), channel_id=1, replica_groups=mesh['grp'=8,'mem'=4] {'grp'}, use_global_device_ids=true, to_apply=%region_8.0 | all-reduce | flops 64 | bytes 512 | tf_op jit(solution)/shard_map/psum | solution.py:83
  405.8 3.6 fusion.364
  419.0 9.7 %collective-permute-done.5 = f32[64,2048]{1,0:T(8,128)} collective-permute-done((f32[64,2048]{1,0:T(8,128)}, f32[64,2048]{1,0:T(8,128)}, u32[]{:S(2)}, u32[]{:S(2)}) %collective-permute-start.5) | collective-permute-done | bytes 524320 | tf_op jit(solution)/shard_map/ppermute | solution.py:14
  431.2 36.1 %all-reduce.7.cloned.1.call-done = f32[2048,64]{0,1:T(8,128)} async-done(((f32[2048,64]{0,1:T(8,128)}), f32[2048,64]{0,1:T(8,128)}) %all-reduce.7.cloned.1.call-update) | async-done | bytes 524304 | tf_op jit(solution)/shard_map/psum | solution.py:72
  538.2 12.3 %collective-permute-done.7 = f32[64,2048]{1,0:T(8,128)S(1)} collective-permute-done((f32[64,2048]{1,0:T(8,128)S(1)}, f32[64,2048]{1,0:T(8,128)S(1)}, u32[]{:S(2)}, u32[]{:S(2)}) %collective-permute-start.7) | collective-permute-done | bytes 524320 | tf_op jit(solution)/shard_map/ppermute | solution.py:26
  553.7 3.2 copy.35
  563.4 39.3 %psum.97 = f32[64]{0:T(128)S(1)} all-reduce(f32[64]{0:T(128)S(1)} %get-tuple-element.479), channel_id=1, replica_groups=mesh['grp'=8,'mem'=4] {'grp','mem'}, use_global_device_ids=true, to_apply=%region_12.0 | all-reduce | flops 64 | bytes 512 | tf_op jit(solution)/shard_map/psum | solution.py:77
  606.1 10.2 %psum.98 = f32[64]{0:T(128)S(1)} all-reduce(f32[64]{0:T(128)S(1)} %get-tuple-element.481), channel_id=1, replica_groups=mesh['grp'=8,'mem'=4] {'mem'}, use_global_device_ids=true, to_apply=%region_14.0 | all-reduce | flops 64 | bytes 512 | tf_op jit(solution)/shard_map/psum | solution.py:83
  616.3 11.8 %psum.99 = f32[64]{0:T(128)S(1)} all-reduce(f32[64]{0:T(128)S(1)} %psum.98), channel_id=1, replica_groups=mesh['grp'=8,'mem'=4] {'grp'}, use_global_device_ids=true, to_apply=%region_15.0 | all-reduce | flops 64 | bytes 512 | tf_op jit(solution)/shard_map/psum | solution.py:83
  634.1 3.6 fusion.363
  647.5 9.3 %collective-permute-done.9 = f32[64,2048]{1,0:T(8,128)} collective-permute-done((f32[64,2048]{1,0:T(8,128)}, f32[64,2048]{1,0:T(8,128)}, u32[]{:S(2)}, u32[]{:S(2)}) %collective-permute-start.9) | collective-permute-done | bytes 524320 | tf_op jit(solution)/shard_map/ppermute | solution.py:14
  659.0 37.4 %all-reduce.9.cloned.1.call-done = f32[2048,64]{0,1:T(8,128)} async-done(((f32[2048,64]{0,1:T(8,128)}), f32[2048,64]{0,1:T(8,128)}) %all-reduce.9.cloned.1.call-update) | async-done | bytes 524304 | tf_op jit(solution)/shard_map/psum | solution.py:72
  767.0 12.2 %collective-permute-done.11 = f32[64,2048]{1,0:T(8,128)S(1)} collective-permute-done((f32[64,2048]{1,0:T(8,128)S(1)}, f32[64,2048]{1,0:T(8,128)S(1)}, u32[]{:S(2)}, u32[]{:S(2)}) %collective-permute-start.11) | collective-permute-done | bytes 524320 | tf_op jit(solution)/shard_map/ppermute | solution.py:26
  782.5 3.2 copy.39
  791.4 39.3 %psum.101 = f32[64]{0:T(128)S(1)} all-reduce(f32[64]{0:T(128)S(1)} %get-tuple-element.521), channel_id=1, replica_groups=mesh['grp'=8,'mem'=4] {'grp','mem'}, use_global_device_ids=true, to_apply=%region_19.0 | all-reduce | flops 64 | bytes 512 | tf_op jit(solution)/shard_map/psum | solution.py:77
  832.4 10.2 %psum.102 = f32[64]{0:T(128)S(1)} all-reduce(f32[64]{0:T(128)S(1)} %get-tuple-element.523), channel_id=1, replica_groups=mesh['grp'=8,'mem'=4] {'mem'}, use_global_device_ids=true, to_apply=%region_21.0 | all-reduce | flops 64 | bytes 512 | tf_op jit(solution)/shard_map/psum | solution.py:83
  842.6 11.8 %psum.103 = f32[64]{0:T(128)S(1)} all-reduce(f32[64]{0:T(128)S(1)} %psum.102), channel_id=1, replica_groups=mesh['grp'=8,'mem'=4] {'grp'}, use_global_device_ids=true, to_apply=%region_22.0 | all-reduce | flops 64 | bytes 512 | tf_op jit(solution)/shard_map/psum | solution.py:83
  (679 shorter events, 345.8 us)
Async XLA Ops:
  7.2 1.2 copy-start
  7.2 246.9 %all-reduce.5.cloned.1.call-start = ((), (), s32[]{:S(2)}) async-start(), calls=%async_computation | async-start | bytes 1048576 | tf_op jit(solution)/shard_map/psum | solution.py:72
  19.5 16.1 %collective-permute-start.1 = (f32[64,2048]{1,0:T(8,128)}, f32[64,2048]{1,0:T(8,128)}, u32[]{:S(2)}, u32[]{:S(2)}) collective-permute-start(f32[64,2048]{1,0:T(8,128)} %copy.30), channel_id=1, source_target_pairs={{28,0},{0,4},{4,8},{8,12},{12,16},{16,20},{20,24},{24,28},{29,1},{... | collective-permute-start | bytes 1572872 | tf_op jit(solution)/shard_map/ppermute | solution.py:14
  21.1 14.5 %collective-permute-start = (f32[64,2048]{1,0:T(8,128)}, f32[64,2048]{1,0:T(8,128)S(1)}, u32[]{:S(2)}, u32[]{:S(2)}) collective-permute-start(f32[64,2048]{1,0:T(8,128)} %copy.29), channel_id=1, source_target_pairs={{4,0},{8,4},{12,8},{16,12},{20,16},{24,20},{28,24},{0,28},{5,1},{9... | collective-permute-start | bytes 1572872 | tf_op jit(solution)/shard_map/ppermute | solution.py:14
  37.6 429.8 %all-reduce.7.cloned.1.call-start = ((), (), s32[]{:S(2)}) async-start(), calls=%async_computation.1 | async-start | bytes 1048576 | tf_op jit(solution)/shard_map/psum | solution.py:72
  254.1 39.4 %copy-start.1 = (f32[2048,2048]{1,0:T(8,128)S(1)}, f32[2048,2048]{1,0:T(8,128)}, u32[]{:S(2)}) copy-start(f32[2048,2048]{1,0:T(8,128)} %get-tuple-element.572) | copy-start | bytes 50331652
  274.3 35.6 %copy-start.2 = (bf16[8,256,256]{2,1,0:T(8,128)(2,1)S(1)}, bf16[8,256,256]{2,1,0:T(8,128)(2,1)}, u32[]{:S(2)}) copy-start(bf16[8,256,256]{2,1,0:T(8,128)(2,1)} %param.14) | copy-start | bytes 3145732
  274.4 35.6 %copy-start.9 = (f32[8,64,256]{2,1,0:T(8,128)S(1)}, f32[8,64,256]{2,1,0:T(8,128)}, u32[]{:S(2)}) copy-start(f32[8,64,256]{2,1,0:T(8,128)} %param.11) | copy-start | bytes 1572868
  294.6 35.9 %copy-start.7 = (bf16[8,24,256]{2,1,0:T(8,128)(2,1)S(1)}, bf16[8,24,256]{2,1,0:T(8,128)(2,1)}, u32[]{:S(2)}) copy-start(bf16[8,24,256]{2,1,0:T(8,128)(2,1)} %param.15) | copy-start | bytes 294916
  308.3 14.0 %collective-permute-start.3 = (f32[64,2048]{1,0:T(8,128)S(1)}, f32[64,2048]{1,0:T(8,128)S(1)}, u32[]{:S(2)}, u32[]{:S(2)}) collective-permute-start(f32[64,2048]{1,0:T(8,128)S(1)} %bitcast.583), channel_id=1, source_target_pairs={{4,0},{8,4},{12,8},{16,12},{20,16},{24,20},{28,24},{0,28},{5,1},{9... | collective-permute-start | bytes 1572872 | tf_op jit(solution)/shard_map/ppermute | solution.py:26
  310.0 13.5 %collective-permute-start.2 = (f32[64,2048]{1,0:T(8,128)S(1)}, f32[64,2048]{1,0:T(8,128)S(1)}, u32[]{:S(2)}, u32[]{:S(2)}) collective-permute-start(f32[64,2048]{1,0:T(8,128)S(1)} %bitcast.584), channel_id=1, source_target_pairs={{0,4},{4,8},{8,12},{12,16},{16,20},{20,24},{24,28},{28,0},{1,5},{5... | collective-permute-start | bytes 1572872 | tf_op jit(solution)/shard_map/ppermute | solution.py:24
  375.3 0.8 copy-start.6
  401.2 0.8 copy-start.4
  414.0 14.7 %collective-permute-start.5 = (f32[64,2048]{1,0:T(8,128)}, f32[64,2048]{1,0:T(8,128)}, u32[]{:S(2)}, u32[]{:S(2)}) collective-permute-start(f32[64,2048]{1,0:T(8,128)} %copy.34), channel_id=1, source_target_pairs={{28,0},{0,4},{4,8},{8,12},{12,16},{16,20},{20,24},{24,28},{29,1},{... | collective-permute-start | bytes 1572872 | tf_op jit(solution)/shard_map/ppermute | solution.py:14
  414.4 14.3 %collective-permute-start.4 = (f32[64,2048]{1,0:T(8,128)}, f32[64,2048]{1,0:T(8,128)}, u32[]{:S(2)}, u32[]{:S(2)}) collective-permute-start(f32[64,2048]{1,0:T(8,128)} %copy.33), channel_id=1, source_target_pairs={{4,0},{8,4},{12,8},{16,12},{20,16},{24,20},{28,24},{0,28},{5,1},{9... | collective-permute-start | bytes 1572872 | tf_op jit(solution)/shard_map/ppermute | solution.py:14
  431.0 265.4 %all-reduce.9.cloned.1.call-start = ((), (), s32[]{:S(2)}) async-start(), calls=%async_computation.2 | async-start | bytes 1048576 | tf_op jit(solution)/shard_map/psum | solution.py:72
  537.2 13.2 %collective-permute-start.7 = (f32[64,2048]{1,0:T(8,128)S(1)}, f32[64,2048]{1,0:T(8,128)S(1)}, u32[]{:S(2)}, u32[]{:S(2)}) collective-permute-start(f32[64,2048]{1,0:T(8,128)S(1)} %bitcast.586), channel_id=1, source_target_pairs={{4,0},{8,4},{12,8},{16,12},{20,16},{24,20},{28,24},{0,28},{5,1},{9... | collective-permute-start | bytes 1572872 | tf_op jit(solution)/shard_map/ppermute | solution.py:26
  538.2 14.2 %collective-permute-start.6 = (f32[64,2048]{1,0:T(8,128)S(1)}, f32[64,2048]{1,0:T(8,128)S(1)}, u32[]{:S(2)}, u32[]{:S(2)}) collective-permute-start(f32[64,2048]{1,0:T(8,128)S(1)} %bitcast.587), channel_id=1, source_target_pairs={{0,4},{4,8},{8,12},{12,16},{16,20},{20,24},{24,28},{28,0},{1,5},{5... | collective-permute-start | bytes 1572872 | tf_op jit(solution)/shard_map/ppermute | solution.py:24
  604.0 0.8 copy-start.5
  642.3 14.4 %collective-permute-start.9 = (f32[64,2048]{1,0:T(8,128)}, f32[64,2048]{1,0:T(8,128)}, u32[]{:S(2)}, u32[]{:S(2)}) collective-permute-start(f32[64,2048]{1,0:T(8,128)} %copy.38), channel_id=1, source_target_pairs={{28,0},{0,4},{4,8},{8,12},{12,16},{16,20},{20,24},{24,28},{29,1},{... | collective-permute-start | bytes 1572872 | tf_op jit(solution)/shard_map/ppermute | solution.py:14
  642.3 14.4 %collective-permute-start.8 = (f32[64,2048]{1,0:T(8,128)}, f32[64,2048]{1,0:T(8,128)}, u32[]{:S(2)}, u32[]{:S(2)}) collective-permute-start(f32[64,2048]{1,0:T(8,128)} %copy.37), channel_id=1, source_target_pairs={{4,0},{8,4},{12,8},{16,12},{20,16},{24,20},{28,24},{0,28},{5,1},{9... | collective-permute-start | bytes 1572872 | tf_op jit(solution)/shard_map/ppermute | solution.py:14
  766.0 13.2 %collective-permute-start.11 = (f32[64,2048]{1,0:T(8,128)S(1)}, f32[64,2048]{1,0:T(8,128)S(1)}, u32[]{:S(2)}, u32[]{:S(2)}) collective-permute-start(f32[64,2048]{1,0:T(8,128)S(1)} %bitcast.580), channel_id=1, source_target_pairs={{4,0},{8,4},{12,8},{16,12},{20,16},{24,20},{28,24},{0,28},{5,1},{9... | collective-permute-start | bytes 1572872 | tf_op jit(solution)/shard_map/ppermute | solution.py:26
  767.0 14.3 %collective-permute-start.10 = (f32[64,2048]{1,0:T(8,128)S(1)}, f32[64,2048]{1,0:T(8,128)S(1)}, u32[]{:S(2)}, u32[]{:S(2)}) collective-permute-start(f32[64,2048]{1,0:T(8,128)S(1)} %bitcast.581), channel_id=1, source_target_pairs={{0,4},{4,8},{8,12},{12,16},{16,20},{20,24},{24,28},{28,0},{1,5},{5... | collective-permute-start | bytes 1572872 | tf_op jit(solution)/shard_map/ppermute | solution.py:24
  831.8 25.1 %copy-start.8 = (f32[8,64,256]{2,1,0:T(8,128)}, f32[8,64,256]{2,1,0:T(8,128)S(1)}, u32[]{:S(2)}) copy-start(f32[8,64,256]{2,1,0:T(8,128)S(1)} %multiply_subtract_fusion) | copy-start | bytes 1572868
  (1 other events, 0.8 us)
Sparse Core Ops, SparseCore 0:
  37.7 39.6 all-reduce.4
  431.1 36.2 all-reduce.6
  659.1 37.2 all-reduce.8
